TPU v7x, 512 devices: a whole 4x8x8 slice. The times are simulated.
512 devices in a mesh: vocab: 64 (over y, x, core), grp: 8 (over z).
Axes of the slice: x: 4, y: 8, z: 8, core: 2. Of those that a mesh axis runs over, the one named last changes fastest.
Arguments:
- hidden: bfloat16 [2048, 4096], P('grp'), may hold values from -240 to 240
- head_weight: bfloat16 [4096, 32768], P('grp', 'vocab'), may hold values from -0.25 to 0.25
- cluster_weight: bfloat16 [4096, 3], replicated, may hold values from -0.5 to 0.5
- proj_one: bfloat16 [4096, 1024], P('vocab'), may hold values from -0.09375 to 0.09375
- proj_two: bfloat16 [4096, 256], P('vocab'), may hold values from -0.09375 to 0.09375
- proj_three: bfloat16 [4096, 64], P('vocab'), may hold values from -0.09375 to 0.09375
- tail_one: bfloat16 [1024, 65536], P('grp', 'vocab'), may hold values from -0.5 to 0.5
- tail_two: bfloat16 [256, 65536], P('grp', 'vocab'), may hold values from -1 to 1
- tail_three: bfloat16 [64, 65536], P('grp', 'vocab'), may hold values from -2 to 2
- targets: int32 [2048], P('grp'), may hold values from 0 to 229375, as said below
- flags: int32 [2048, 3], P('grp'), may hold values from 0 to 1, as said below
Outputs:
- target_logprob: float32 [2048], P('grp')
- tail_entropy: float32 [2048, 3], P('grp')
Inputs may be any that keep to these rules, and one draw needn't show every extreme that they name: `targets`: a target at or beyond 32768 lies in tail (t - 32768) // 65536. flags[b, c] is 1 whenever the target of sequence b lies in tail c.
All inputs are finite; a program needn't handle non-finite values.
Results may differ from a plain program's by a relative error of at most 0.0092.
Values may be sent and summed in bfloat16 or wider, within the bound.
No kernel may reach another device: no remote copies, remote signals or barrier semaphores. Data moves between devices by JAX's collectives and lax.ppermute only.
A program may use at most 64 MiB of HBM per device.

v0:
```python
import jax
import jax.numpy as jnp
from jax import lax
from jax.sharding import Mesh
from jax.sharding import PartitionSpec as P

V_HEAD = 32768
TAIL = 65536
VOCAB = ("vocab_0", "vocab_1", "vocab_2")


def split_up(shard, dim, size):
    dims = shard.shape
    pieces = shard.reshape(*dims[:dim], size, dims[dim] // size, *dims[dim + 1 :])
    return jnp.moveaxis(pieces, dim, 0)


def sent_and_summed(shard, axis, dim):
    pieces = split_up(shard, dim, lax.axis_size(axis))
    arrived = lax.all_to_all(pieces, axis, split_axis=0, concat_axis=0, tiled=True)
    return arrived.sum(axis=0)


def laid_out(pieces, dim):
    pieces = jnp.moveaxis(pieces, 0, dim)
    dims = pieces.shape
    return pieces.reshape(*dims[:dim], dims[dim] * dims[dim + 1], *dims[dim + 2 :])


def copy_for_each(shard, axis):
    copies = jnp.broadcast_to(shard, (lax.axis_size(axis), *shard.shape))
    return lax.all_to_all(copies, axis, split_axis=0, concat_axis=0, tiled=True)


def gathered_copies(shard, axis, dim):
    return laid_out(copy_for_each(shard, axis), dim)


def one_gather(arrays, axis, dims):
    vector = jnp.concatenate([a.reshape(-1) for a in arrays])
    lines, at, done = (lax.all_gather(vector, axis), 0, [])
    for a, dim in zip(arrays, dims):
        pieces = lines[:, at : at + a.size].reshape(-1, *a.shape)
        done.append(laid_out(pieces, dim))
        at += a.size
    return tuple(done)


def collected_together(shard, axis):
    leaves = jax.tree.leaves(shard)
    order = sorted(range(len(leaves)), key=lambda k: -leaves[k].size)
    width = (1, *leaves[order[0]].shape)[-1]
    lines = [
        jnp.pad(leaves[k].reshape(-1), (0, -leaves[k].size % width)).reshape(-1, width)
        for k in order
    ]
    both, at, found = (lax.all_gather(jnp.concatenate(lines), axis), 0, {})
    for k, line in zip(order, lines):
        share = both[:, at : at + len(line)].reshape(len(both), -1)
        found[k] = share[:, : leaves[k].size].reshape(-1, *leaves[k].shape)
        at += len(line)
    numbers = iter(range(len(leaves)))
    return jax.tree.map(lambda _: found[next(numbers)], shard)


def combined_by_axis(shard, axes, combine):
    for axis in axes:
        pieces = collected_together(shard, axis)
        shard = jax.tree.map(lambda part: part[0], pieces)
        for k in range(1, lax.axis_size(axis)):
            shard = combine(shard, jax.tree.map(lambda part: part[k], pieces))
    return shard


def combine_stats(first, second):
    head_max = jnp.maximum(first[0], second[0])
    head_sum = first[1] * jnp.exp(first[0] - head_max) + second[1] * jnp.exp(second[0] - head_max)
    tail_max = jnp.maximum(first[2], second[2])
    left = jnp.exp(first[2] - tail_max)
    right = jnp.exp(second[2] - tail_max)
    tail_sum = first[3] * left + second[3] * right
    tail_weighted = first[4] * left + second[4] * right
    return (head_max, head_sum, tail_max, tail_sum, tail_weighted, first[5] + second[5])


def shards(
    hidden,
    head_weight,
    cluster_weight,
    proj_one,
    proj_two,
    proj_three,
    tail_one,
    tail_two,
    tail_three,
    targets,
    flags,
):
    rows = hidden.shape[0]
    head_cols = head_weight.shape[1]
    vocab_index = lax.axis_index(VOCAB)
    head_logits = jnp.dot(
        hidden,
        lax.all_gather(head_weight, "grp", axis=0, tiled=True),
        preferred_element_type=jnp.float32,
    )
    cluster_score_logits = jnp.dot(hidden, cluster_weight, preferred_element_type=jnp.float32)
    width_voc = proj_one.shape[0]
    features = lax.dynamic_slice_in_dim(hidden, vocab_index * width_voc, width_voc, 1)
    joined_weight = jnp.concatenate((proj_one, proj_two, proj_three), axis=1)
    joined_partial_logits = jnp.dot(features, joined_weight, preferred_element_type=jnp.float32)
    share = sent_and_summed(joined_partial_logits, VOCAB, 1).astype(jnp.bfloat16)
    joined = gathered_copies(share, VOCAB, 1)
    first_end = proj_one.shape[1]
    second_end = first_end + proj_two.shape[1]
    projected = [joined[:, :first_end], joined[:, first_end:second_end], joined[:, second_end:]]
    full_tails = one_gather((tail_one, tail_two, tail_three), "grp", (0, 0, 0))
    tail_cluster_logits = jnp.stack(
        [
            jnp.dot(projected[index], full_tails[index], preferred_element_type=jnp.float32)
            for index in range(3)
        ],
        axis=0,
    )
    tail_cols = tail_cluster_logits.shape[2]
    head_ids = vocab_index * head_cols + jnp.arange(head_cols, dtype=jnp.int32)
    head_pick = jnp.sum(jnp.where(head_ids[None, :] == targets[:, None], head_logits, 0.0), axis=1)
    relative = targets - V_HEAD
    cluster = relative // TAIL
    word = relative - cluster * TAIL
    tail_ids = vocab_index * tail_cols + jnp.arange(tail_cols, dtype=jnp.int32)
    same_word = tail_ids[None, :] == word[:, None]
    tail_pick = jnp.zeros((rows,), jnp.float32)
    for index in range(3):
        hit = jnp.logical_and(same_word, (cluster == index)[:, None])
        tail_pick = tail_pick + jnp.sum(jnp.where(hit, tail_cluster_logits[index], 0.0), axis=1)
    picked = head_pick + tail_pick
    local_head_max = jnp.max(head_logits, axis=1)
    local_tail_max = jnp.transpose(jnp.max(tail_cluster_logits, axis=2))
    head_sum = jnp.sum(jnp.exp(head_logits - local_head_max[:, None]), axis=1)
    expo = jnp.exp(tail_cluster_logits - jnp.transpose(local_tail_max)[:, :, None])
    tail_sum = jnp.transpose(jnp.sum(expo, axis=2))
    tail_weighted = jnp.transpose(jnp.sum(expo * tail_cluster_logits, axis=2))
    merged = combined_by_axis(
        (local_head_max, head_sum, local_tail_max, tail_sum, tail_weighted, picked),
        VOCAB,
        combine_stats,
    )
    head_max, head_sum, tail_max, tail_sum, tail_weighted, picked = merged
    top = jnp.maximum(head_max, jnp.max(cluster_score_logits, axis=1))
    total = head_sum * jnp.exp(head_max - top) + jnp.sum(
        jnp.exp(cluster_score_logits - top[:, None]), axis=1
    )
    head_lse = top + jnp.log(total)
    tail_lse = tail_max + jnp.log(tail_sum)
    tail_mean = tail_weighted / tail_sum
    tail_entropy = flags.astype(jnp.float32) * (tail_lse - tail_mean)
    which = cluster[:, None] == jnp.arange(3, dtype=jnp.int32)[None, :]
    cluster_term = jnp.sum(jnp.where(which, cluster_score_logits - tail_lse, 0.0), axis=1)
    target_logprob = jnp.where(targets < V_HEAD, picked, picked + cluster_term) - head_lse
    return (target_logprob, tail_entropy)


def solution(mesh):
    finer = Mesh(
        mesh.devices.reshape(8, 4, 2, mesh.shape["grp"]), ("vocab_0", "vocab_1", "vocab_2", "grp")
    )
    in_specs = (
        P("grp", None),
        P("grp", VOCAB),
        P(),
        P(VOCAB, None),
        P(VOCAB, None),
        P(VOCAB, None),
        P("grp", VOCAB),
        P("grp", VOCAB),
        P("grp", VOCAB),
        P("grp"),
        P("grp", None),
    )
    out_specs = (P("grp"), P("grp", None))
    return jax.shard_map(
        shards, mesh=finer, in_specs=in_specs, out_specs=out_specs, check_vma=False
    )
```

profile of v0, /device:TPU:1, one launch (start us, length us, event | category | flops | bytes accessed | tf_op | source)
XLA Modules:
  0.0 180.4 jit_solution(7953923734584151872)
XLA Ops:
  7.2 0.9 copy.71
  8.1 0.8 copy.68
  8.9 1.0 copy.67
  9.9 0.8 pad_maximum_fusion.1
  10.8 0.7 all-gather.10.cloned.1.call-update
  11.5 1.4 fusion.4
  12.9 1.3 reshape.130
  14.2 50.8 %all_to_all.10 = f32[64,256,21]{1,2,0:T(8,128)} all-to-all(f32[64,256,21]{1,2,0:T(8,128)} %bitcast.526), channel_id=1, replica_groups=mesh['vocab_0'=8,'vocab_1'=4,'vocab_2'=2,'grp'=8] {'vocab_0','vocab_1','..., dimensions={0} | all-to-all | bytes 2752512 | tf_op jit(solution)/shard_map/all_to_all | solution.py:20
  65.1 1.5 reduce_sum.90
  66.6 0.9 broadcast_in_dim.15
  67.5 6.4 %all-to-all-start.1 = ((bf16[64,256,21]{1,2,0:T(8,128)(2,1)}), bf16[64,256,21]{1,2,0:T(8,128)(2,1)S(1)}, u32[]{:S(2)}, u32[]{:S(2)}) async-start(bf16[64,256,21]{1,2,0:T(8,128)(2,1)} %broadcast_in_dim.15), calls=%async_computation.1 | async-start | bytes 1572864 | tf_op jit(solution)/shard_map/all_to_all | solution.py:32
  74.0 0.7 fusion.112
  74.7 22.2 %all-to-all-done.1 = bf16[64,256,21]{1,2,0:T(8,128)(2,1)S(1)} async-done(((bf16[64,256,21]{1,2,0:T(8,128)(2,1)}), bf16[64,256,21]{1,2,0:T(8,128)(2,1)S(1)}, u32[]{:S(2)}, u32[]{:S(2)}) %all-to-all-start.1) | async-done | bytes 688160 | tf_op jit(solution)/shard_map/all_to_all | solution.py:32
  97.0 1.1 reshape.131
  98.0 4.6 %reshape.156 = bf16[8,172032]{1,0:T(8,128)(2,1)} reshape(bf16[1376256]{0:T(1024)(128)(2,1)} %all-gather.12.cloned.1.call-done) | data formatting | bytes 5505024 | tf_op jit(solution)/shard_map/all_gather | solution.py:41
  102.6 3.1 %slice.499 = bf16[8,131072]{1,0:T(8,128)(2,1)} slice(bf16[8,172032]{1,0:T(8,128)(2,1)} %reshape.156), slice={[0:8], [0:131072]} | slice | bytes 4194304 | tf_op jit(solution)/shard_map/slice | solution.py:43
  105.7 0.7 reshape_reshape.11
  106.4 3.9 %reshape_reshape.9 = bf16[1024,1024]{1,0:T(8,128)(2,1)} reshape(bf16[8,131072]{1,0:T(8,128)(2,1)} %slice.499) | data formatting | bytes 4194304 | tf_op jit(solution)/shard_map/reshape;reshape | solution.py:27
  110.4 1.0 reshape_reshape.10
  111.4 0.3 fusion.14
  111.7 2.3 %fusion.2 = f32[256,1024]{1,0:T(8,128)S(1)} fusion(bf16[1024,1024]{1,0:T(8,128)(2,1)} %reshape_reshape.9, bf16[256,1344]{0,1:T(8,128)(2,1)S(1)} %copy-done.1), kind=kOutput, calls=%fused_computation.11 | convolution fusion | flops 536870912 | bytes 3670016 | tf_op jit(solution)/shard_map/dot_general | solution.py:120
  114.1 0.8 select_reduce_fusion.1
  115.0 0.9 multiply_reduce_fusion
  115.9 5.0 %all-gather.10.cloned.1.call-done = bf16[4096,512]{1,0:T(8,128)(2,1)} async-done(((bf16[512,512]{1,0:T(8,128)(2,1)}), bf16[4096,512]{1,0:T(8,128)(2,1)}) %all-gather.10.cloned.1.call-update) | async-done | bytes 4194320 | tf_op jit(solution)/shard_map/all_gather | solution.py:104
  120.9 3.5 %fusion.111 = (f32[256]{0:T(256)S(1)}, f32[256,512]{1,0:T(8,128)S(1)}) fusion(bf16[256,4096]{1,0:T(8,128)(2,1)S(1)} %copy-done, bf16[4096,512]{1,0:T(8,128)(2,1)} %all-gather.10.cloned.1.call-done), kind=kOutput, calls=%fused_computation.231 | convolution fusion | flops 1073872640 | bytes 6816768 | tf_op jit(solution)/shard_map/dot_general | solution.py:102
  125.6 19.9 %all-gather.4 = f32[8,1026,3]{1,2,0:T(4,128)S(1)} all-gather(f32[1,1026,3]{1,2,0:T(4,128)S(1)} %bitcast.534), channel_id=3, replica_groups=mesh['vocab_0'=8,'vocab_1'=4,'vocab_2'=2,'grp'=8] {'vocab_0'}, dimensions={0}, use_global_device_ids=true | all-gather | bytes 110808 | tf_op jit(solution)/shard_map/all_gather | solution.py:57
  145.9 0.4 fusion.10
  147.0 1.1 slice_reduce_fusion.7
  148.8 9.3 %all-gather.5 = f32[4,1026,3]{1,2,0:T(4,128)S(1)} all-gather(f32[1,1026,3]{1,2,0:T(4,128)S(1)} %bitcast.535), channel_id=4, replica_groups=mesh['vocab_0'=8,'vocab_1'=4,'vocab_2'=2,'grp'=8] {'vocab_1'}, dimensions={0}, use_global_device_ids=true | all-gather | bytes 61560 | tf_op jit(solution)/shard_map/all_gather | solution.py:57
  160.2 11.1 %all-gather.6 = f32[2,1026,3]{1,2,0:T(4,128)S(1)} all-gather(f32[1,1026,3]{1,2,0:T(4,128)S(1)} %bitcast.533), channel_id=5, replica_groups=mesh['vocab_0'=8,'vocab_1'=4,'vocab_2'=2,'grp'=8] {'vocab_2'}, dimensions={0}, use_global_device_ids=true | all-gather | bytes 36936 | tf_op jit(solution)/shard_map/all_gather | solution.py:57
  172.3 0.6 exponential_reduce_fusion.1
  173.0 0.6 fusion.95
  (96 shorter events, 6.2 us)
Async XLA Ops:
  7.2 4.3 %copy-start = (bf16[256,4096]{1,0:T(8,128)(2,1)S(1)}, bf16[256,4096]{1,0:T(8,128)(2,1)}, u32[]{:S(2)}) copy-start(bf16[256,4096]{1,0:T(8,128)(2,1)} %param.11) | copy-start | bytes 6291460
  7.2 90.9 %all-gather.12.cloned.1.call-start = ((), (), s32[]{:S(2)}) async-start(), calls=%async_computation.3 | async-start | bytes 3096576 | tf_op jit(solution)/shard_map/all_gather | solution.py:41
  10.7 110.2 %all-gather.10.cloned.1.call-start = ((), (), s32[]{:S(2)}) async-start(), calls=%async_computation.2 | async-start | bytes 4718592 | tf_op jit(solution)/shard_map/all_gather | solution.py:104
  65.1 8.9 %copy-start.5 = (s32[256]{0:T(256)S(1)}, s32[256]{0:T(256)}, u32[]{:S(2)}) copy-start(s32[256]{0:T(256)} %param.20) | copy-start | bytes 3076
  65.1 9.0 %copy-start.4 = (bf16[4096,3]{0,1:T(4,128)(2,1)S(1)}, bf16[4096,3]{0,1:T(4,128)(2,1)}, u32[]{:S(2)}) copy-start(bf16[4096,3]{0,1:T(4,128)(2,1)} %param.13) | copy-start | bytes 73732
  67.5 29.4 %all-to-all-start.1 = ((bf16[64,256,21]{1,2,0:T(8,128)(2,1)}), bf16[64,256,21]{1,2,0:T(8,128)(2,1)S(1)}, u32[]{:S(2)}, u32[]{:S(2)}) async-start(bf16[64,256,21]{1,2,0:T(8,128)(2,1)} %broadcast_in_dim.15), calls=%async_computation.1 | async-start | bytes 1572864 | tf_op jit(solution)/shard_map/all_to_all | solution.py:32
  102.6 3.1 %slice-start = ((bf16[8,172032]{1,0:T(8,128)(2,1)}), bf16[8,8192]{1,0:T(8,128)(2,1)S(1)}, s32[]{:S(2)}) async-start(bf16[8,172032]{1,0:T(8,128)(2,1)} %reshape.156), calls=%async_computation.4 | async-start | bytes 262144 | tf_op jit(solution)/shard_map/slice | solution.py:43
  105.7 4.6 %slice-start.1 = ((bf16[8,172032]{1,0:T(8,128)(2,1)}), bf16[8,32768]{1,0:T(8,128)(2,1)S(1)}, s32[]{:S(2)}) async-start(bf16[8,172032]{1,0:T(8,128)(2,1)} %reshape.156), calls=%async_computation.5 | async-start | bytes 1048576 | tf_op jit(solution)/shard_map/slice | solution.py:43
  105.7 5.7 %copy-start.1 = (bf16[256,1344]{0,1:T(8,128)(2,1)S(1)}, bf16[256,1344]{0,1:T(8,128)(2,1)}, u32[]{:S(2)}) copy-start(bf16[256,1344]{0,1:T(8,128)(2,1)} %reshape.131) | copy-start | bytes 2064388
  106.4 5.0 %copy-start.2 = (bf16[64,1024]{1,0:T(8,128)(2,1)S(1)}, bf16[64,1024]{1,0:T(8,128)(2,1)}, u32[]{:S(2)}) copy-start(bf16[64,1024]{1,0:T(8,128)(2,1)} %reshape_reshape.11) | copy-start | bytes 393220
  111.4 2.6 %copy-start.3 = (bf16[256,1024]{1,0:T(8,128)(2,1)S(1)}, bf16[256,1024]{1,0:T(8,128)(2,1)}, u32[]{:S(2)}) copy-start(bf16[256,1024]{1,0:T(8,128)(2,1)} %reshape_reshape.10) | copy-start | bytes 1572868
  146.7 25.6 %copy-start.6 = (s32[256,3]{0,1:T(4,128)S(1)}, s32[256,3]{0,1:T(4,128)}, u32[]{:S(2)}) copy-start(s32[256,3]{0,1:T(4,128)} %param.21) | copy-start | bytes 9220
Sparse Core Ops, SparseCore 0:
  10.8 48.8 all-gather.11
  61.8 59.1 all-gather.9
where the time goes:
time: 181 us; the launch traced here: 180 us
  blocking collectives  91.2 us (50%)
  waiting for transfers between devices  27.9 us (15%)
  local copies, waits for them, and re-layouts  25.9 us (14%)
  between operations  14.4 us (8%)
  matrix products  8.93 us (5%)
  starting transfers between devices  6.48 us (4%)
  other arithmetic  5.55 us (3%)
    all_to_all x1, blocking collectives, sent_and_summed(): lax.all_to_all(pieces, axis, split_axis=0, concat_axis=0, tiled=True)  50.8 us
    all_gather x3, blocking collectives, collected_together(): both, at, found = (lax.all_gather(jnp.concatenate(lines), axis), 0, {})  40.3 us
    all_to_all x1, waiting for transfers between devices, copy_for_each(): return lax.all_to_all(copies, axis, split_axis=0, concat_axis=0, tiled=True)  22.2 us
    all_to_all x1, starting transfers between devices, copy_for_each(): return lax.all_to_all(copies, axis, split_axis=0, concat_axis=0, tiled=True)  6.4 us
    another operation x3, local copies, waits for them, and re-layouts, laid_out(): pieces.reshape(*dims[:dim], dims[dim] * dims[dim + 1], *dims[dim + 2:])  5.69 us
    all_gather x1, waiting for transfers between devices, shards(): lax.all_gather(head_weight, 'grp', axis=0, tiled=True)  4.98 us
    all_gather x1, local copies, waits for them, and re-layouts, one_gather(): lines, at, done = (lax.all_gather(vector, axis), 0, [])  4.56 us
  transfers between devices with their start and end apart: 3, of which 2 were waited for; matrix products, arithmetic and copies ran while one was open for 14% of the time, Pallas kernels for 0%

commit v1 on v0

--- a/solution.py
+++ b/solution.py
@@ -101,7 +101,9 @@
     vocab_index = lax.axis_index(VOCAB)
     head_logits = jnp.dot(
         hidden,
-        lax.all_gather(head_weight, "grp", axis=0, tiled=True),
+        jnp.concatenate(
+            lax.all_to_all(jnp.stack([head_weight] * lax.axis_size("grp")), "grp", 0, 0), axis=0
+        ),
         preferred_element_type=jnp.float32,
     )
     cluster_score_logits = jnp.dot(hidden, cluster_weight, preferred_element_type=jnp.float32)

time: 181 us -> 298 us (1.65)
  the two profiles are of different devices: /device:TPU:1 before, /device:TPU:257 now
where the time goes in v1:
time: 298 us; the launch traced here: 297 us
  waiting for transfers between devices  126 us (42%)
  blocking collectives  102 us (34%)
  local copies, waits for them, and re-layouts  28.2 us (9%)
  between operations  14.5 us (5%)
  starting transfers between devices  13.2 us (4%)
  matrix products  8.93 us (3%)
  other arithmetic  5.58 us (2%)
    all_gather x1, waiting for transfers between devices, one_gather(): lines, at, done = (lax.all_gather(vector, axis), 0, [])  103 us
    all_gather x3, blocking collectives, collected_together(): both, at, found = (lax.all_gather(jnp.concatenate(lines), axis), 0, {})  51.6 us
    all_to_all x1, blocking collectives, sent_and_summed(): lax.all_to_all(pieces, axis, split_axis=0, concat_axis=0, tiled=True)  50 us
    all_to_all x1, waiting for transfers between devices, copy_for_each(): return lax.all_to_all(copies, axis, split_axis=0, concat_axis=0, tiled=True)  22.9 us
    all_to_all x1, starting transfers between devices, shards(): lax.all_to_all(jnp.stack([head_weight] * lax.axis_size('grp')), 'grp', 0, 0)  6.81 us
    all_to_all x1, starting transfers between devices, copy_for_each(): return lax.all_to_all(copies, axis, split_axis=0, concat_axis=0, tiled=True)  6.37 us
  transfers between devices with their start and end apart: 3, of which 2 were waited for; matrix products, arithmetic and copies ran while one was open for 7% of the time, Pallas kernels for 0%

profile of v1, /device:TPU:257, one launch (start us, length us, event | category | flops | bytes accessed | tf_op | source)
XLA Modules:
  0.0 297.5 jit_solution(3328314030173060069)
XLA Ops:
  7.2 1.6 copy-done
  8.8 1.4 fusion.4
  10.1 1.3 reshape.135
  11.5 50.0 %all_to_all.15 = f32[64,256,21]{1,2,0:T(8,128)} all-to-all(f32[64,256,21]{1,2,0:T(8,128)} %bitcast.527), channel_id=1, replica_groups=mesh['vocab_0'=8,'vocab_1'=4,'vocab_2'=2,'grp'=8] {'vocab_0','vocab_1','..., dimensions={0} | all-to-all | bytes 2752512 | tf_op jit(solution)/shard_map/all_to_all | solution.py:20
  61.4 1.6 reduce_sum.90
  63.0 0.9 broadcast_in_dim.15
  63.9 6.4 %all-to-all-start.1 = ((bf16[64,256,21]{1,2,0:T(8,128)(2,1)}), bf16[64,256,21]{1,2,0:T(8,128)(2,1)S(1)}, u32[]{:S(2)}, u32[]{:S(2)}) async-start(bf16[64,256,21]{1,2,0:T(8,128)(2,1)} %broadcast_in_dim.15), calls=%async_computation.1 | async-start | bytes 1572864 | tf_op jit(solution)/shard_map/all_to_all | solution.py:32
  70.4 22.9 %all-to-all-done.1 = bf16[64,256,21]{1,2,0:T(8,128)(2,1)S(1)} async-done(((bf16[64,256,21]{1,2,0:T(8,128)(2,1)}), bf16[64,256,21]{1,2,0:T(8,128)(2,1)S(1)}, u32[]{:S(2)}, u32[]{:S(2)}) %all-to-all-start.1) | async-done | bytes 688160 | tf_op jit(solution)/shard_map/all_to_all | solution.py:32
  93.3 3.4 %stack.27 = bf16[8,512,512]{2,1,0:T(8,128)(2,1)} broadcast(bf16[512,512]{1,0:T(8,128)(2,1)} %param.12), dimensions={1,2} | broadcast | bytes 4718592 | tf_op jit(solution)/shard_map/stack | solution.py:105
  96.7 6.8 %all-to-all-start.2 = ((bf16[8,512,512]{2,1,0:T(8,128)(2,1)}), bf16[8,512,512]{2,1,0:T(8,128)(2,1)}, u32[]{:S(2)}, u32[]{:S(2)}) async-start(bf16[8,512,512]{2,1,0:T(8,128)(2,1)} %stack.27), calls=%async_computation.2 | async-start | bytes 8388608 | tf_op jit(solution)/shard_map/all_to_all | solution.py:105
  103.5 0.7 pad_maximum_fusion.1
  104.4 0.7 fusion.112
  105.0 1.1 reshape.136
  106.2 102.7 %all-gather.9.cloned.1.call-done = bf16[1376256]{0:T(1024)(128)(2,1)} async-done(((bf16[172032]{0:T(1024)(128)(2,1)}), bf16[1376256]{0:T(1024)(128)(2,1)}) %all-gather.9.cloned.1.call-update) | async-done | bytes 2752528 | tf_op jit(solution)/shard_map/all_gather | solution.py:41
  208.8 4.6 %reshape.162 = bf16[8,172032]{1,0:T(8,128)(2,1)} reshape(bf16[1376256]{0:T(1024)(128)(2,1)} %all-gather.9.cloned.1.call-done) | data formatting | bytes 5505024 | tf_op jit(solution)/shard_map/all_gather | solution.py:41
  213.4 3.1 %slice.499 = bf16[8,131072]{1,0:T(8,128)(2,1)} slice(bf16[8,172032]{1,0:T(8,128)(2,1)} %reshape.162), slice={[0:8], [0:131072]} | slice | bytes 4194304 | tf_op jit(solution)/shard_map/slice | solution.py:43
  216.5 0.7 reshape_reshape.11
  217.2 3.9 %reshape_reshape.9 = bf16[1024,1024]{1,0:T(8,128)(2,1)} reshape(bf16[8,131072]{1,0:T(8,128)(2,1)} %slice.499) | data formatting | bytes 4194304 | tf_op jit(solution)/shard_map/reshape;reshape | solution.py:27
  221.1 1.1 reshape_reshape.10
  222.2 0.3 fusion.14
  222.5 2.3 fusion.2
  224.8 0.8 select_reduce_fusion.1
  225.8 0.9 multiply_reduce_fusion
  226.7 3.5 %fusion.111 = (f32[256]{0:T(256)S(1)}, f32[256,512]{1,0:T(8,128)S(1)}) fusion(bf16[256,4096]{1,0:T(8,128)(2,1)S(1)} %copy-done, bf16[4096,512]{1,0:T(8,128)(2,1)} %bitcast.8), kind=kOutput, calls=%fused_computation.231 | convolution fusion | flops 1073872640 | bytes 6816768 | tf_op jit(solution)/shard_map/dot_general | solution.py:102
  230.2 0.3 select_reduce_fusion.3
  231.4 31.5 %all-gather.4 = f32[8,1026,3]{1,2,0:T(4,128)S(1)} all-gather(f32[1,1026,3]{1,2,0:T(4,128)S(1)} %bitcast.535), channel_id=3, replica_groups=mesh['vocab_0'=8,'vocab_1'=4,'vocab_2'=2,'grp'=8] {'vocab_0'}, dimensions={0}, use_global_device_ids=true | all-gather | bytes 110808 | tf_op jit(solution)/shard_map/all_gather | solution.py:57
  263.3 0.4 fusion.10
  264.4 1.1 slice_reduce_fusion.7
  266.2 9.0 %all-gather.5 = f32[4,1026,3]{1,2,0:T(4,128)S(1)} all-gather(f32[1,1026,3]{1,2,0:T(4,128)S(1)} %bitcast.536), channel_id=4, replica_groups=mesh['vocab_0'=8,'vocab_1'=4,'vocab_2'=2,'grp'=8] {'vocab_1'}, dimensions={0}, use_global_device_ids=true | all-gather | bytes 61560 | tf_op jit(solution)/shard_map/all_gather | solution.py:57
  277.2 11.1 %all-gather.6 = f32[2,1026,3]{1,2,0:T(4,128)S(1)} all-gather(f32[1,1026,3]{1,2,0:T(4,128)S(1)} %bitcast.534), channel_id=5, replica_groups=mesh['vocab_0'=8,'vocab_1'=4,'vocab_2'=2,'grp'=8] {'vocab_2'}, dimensions={0}, use_global_device_ids=true | all-gather | bytes 36936 | tf_op jit(solution)/shard_map/all_gather | solution.py:57
  289.4 0.6 exponential_reduce_fusion.1
  290.0 0.6 fusion.95
  (102 shorter events, 5.9 us)
Async XLA Ops:
  7.2 1.6 copy-start
  61.4 8.9 %copy-start.8 = (bf16[8,1024]{1,0:T(8,128)(2,1)S(1)}, bf16[8,1024]{1,0:T(8,128)(2,1)}, u32[]{:S(2)}) copy-start(bf16[8,1024]{1,0:T(8,128)(2,1)} %param.19) | copy-start | bytes 49156
  61.4 8.9 %copy-start.5 = (bf16[32,1024]{1,0:T(8,128)(2,1)S(1)}, bf16[32,1024]{1,0:T(8,128)(2,1)}, u32[]{:S(2)}) copy-start(bf16[32,1024]{1,0:T(8,128)(2,1)} %param.18) | copy-start | bytes 196612
  61.4 8.9 %copy-start.4 = (bf16[128,1024]{1,0:T(8,128)(2,1)S(1)}, bf16[128,1024]{1,0:T(8,128)(2,1)}, u32[]{:S(2)}) copy-start(bf16[128,1024]{1,0:T(8,128)(2,1)} %param.17) | copy-start | bytes 786436
  63.9 29.4 %all-to-all-start.1 = ((bf16[64,256,21]{1,2,0:T(8,128)(2,1)}), bf16[64,256,21]{1,2,0:T(8,128)(2,1)S(1)}, u32[]{:S(2)}, u32[]{:S(2)}) async-start(bf16[64,256,21]{1,2,0:T(8,128)(2,1)} %broadcast_in_dim.15), calls=%async_computation.1 | async-start | bytes 1572864 | tf_op jit(solution)/shard_map/all_to_all | solution.py:32
  96.7 7.6 %copy-start.7 = (s32[256]{0:T(256)S(1)}, s32[256]{0:T(256)}, u32[]{:S(2)}) copy-start(s32[256]{0:T(256)} %param.20) | copy-start | bytes 3076
  96.7 7.7 %copy-start.6 = (bf16[4096,3]{0,1:T(4,128)(2,1)S(1)}, bf16[4096,3]{0,1:T(4,128)(2,1)}, u32[]{:S(2)}) copy-start(bf16[4096,3]{0,1:T(4,128)(2,1)} %param.13) | copy-start | bytes 73732
  96.7 130.0 %all-to-all-start.2 = ((bf16[8,512,512]{2,1,0:T(8,128)(2,1)}), bf16[8,512,512]{2,1,0:T(8,128)(2,1)}, u32[]{:S(2)}, u32[]{:S(2)}) async-start(bf16[8,512,512]{2,1,0:T(8,128)(2,1)} %stack.27), calls=%async_computation.2 | async-start | bytes 8388608 | tf_op jit(solution)/shard_map/all_to_all | solution.py:105
  103.5 105.3 %all-gather.9.cloned.1.call-start = ((), (), s32[]{:S(2)}) async-start(), calls=%async_computation.3 | async-start | bytes 3096576 | tf_op jit(solution)/shard_map/all_gather | solution.py:41
  213.4 3.1 %slice-start = ((bf16[8,172032]{1,0:T(8,128)(2,1)}), bf16[8,8192]{1,0:T(8,128)(2,1)S(1)}, s32[]{:S(2)}) async-start(bf16[8,172032]{1,0:T(8,128)(2,1)} %reshape.162), calls=%async_computation.4 | async-start | bytes 262144 | tf_op jit(solution)/shard_map/slice | solution.py:43
  216.4 4.7 %slice-start.1 = ((bf16[8,172032]{1,0:T(8,128)(2,1)}), bf16[8,32768]{1,0:T(8,128)(2,1)S(1)}, s32[]{:S(2)}) async-start(bf16[8,172032]{1,0:T(8,128)(2,1)} %reshape.162), calls=%async_computation.5 | async-start | bytes 1048576 | tf_op jit(solution)/shard_map/slice | solution.py:43
  216.4 5.7 %copy-start.1 = (bf16[256,1344]{0,1:T(8,128)(2,1)S(1)}, bf16[256,1344]{0,1:T(8,128)(2,1)}, u32[]{:S(2)}) copy-start(bf16[256,1344]{0,1:T(8,128)(2,1)} %reshape.136) | copy-start | bytes 2064388
  217.2 5.0 %copy-start.2 = (bf16[64,1024]{1,0:T(8,128)(2,1)S(1)}, bf16[64,1024]{1,0:T(8,128)(2,1)}, u32[]{:S(2)}) copy-start(bf16[64,1024]{1,0:T(8,128)(2,1)} %reshape_reshape.11) | copy-start | bytes 393220
  222.2 2.6 copy-start.3
  264.1 25.3 %copy-start.9 = (s32[256,3]{0,1:T(4,128)S(1)}, s32[256,3]{0,1:T(4,128)}, u32[]{:S(2)}) copy-start(s32[256,3]{0,1:T(4,128)} %param.21) | copy-start | bytes 9220
Sparse Core Ops, SparseCore 0:
  106.4 102.3 all-gather.8
